TPU v7x, 32 devices: a whole 2x2x4 slice. The times are simulated.
32 devices in a mesh: rows: 16 (over z, x, core), feat: 2 (over y).
Axes of the slice: x: 2, y: 2, z: 4, core: 2. Of those that a mesh axis runs over, the one named last changes fastest.
Arguments:
- train_cells: bfloat16 [1024, 1536], P('rows', 'feat'), may hold values from -24 to 24
- test_cells: bfloat16 [512, 1536], P('rows', 'feat'), may hold values from -24 to 24
- feat_weights: bfloat16 [4, 192, 192], replicated
- row_weights: bfloat16 [4, 192, 192], replicated
- mlp_up: bfloat16 [192, 768], replicated, may hold values from -0.4375 to 0.4375
- mlp_down: bfloat16 [768, 192], replicated, may hold values from -0.21875 to 0.21875
Outputs:
- train_out: bfloat16 [1024, 1536], P('rows', 'feat')
- test_out: bfloat16 [512, 1536], P('rows', 'feat')
All inputs are finite; a program needn't handle non-finite values.
Results may differ from a plain program's by a relative error of at most 0.017.
Values may be sent and summed in bfloat16 or wider, within the bound.
A program may use at most 128 MiB of HBM per device.

v0:
```python
import jax
import jax.numpy as jnp
from jax import lax
from jax.sharding import PartitionSpec as P

E = 192
HEADS = 6
HD = 32


eps_norm = 1e-05
far_below = -1e30


def layer_norm(values_in):
    centred = values_in - jnp.mean(values_in, axis=-1, keepdims=True)
    spread = jnp.mean(centred * centred, axis=-1, keepdims=True)
    return centred * lax.rsqrt(spread + eps_norm)


def project(normed, weight):
    height = normed.shape[0]
    return jnp.dot(normed.reshape(-1, E), weight, preferred_element_type=jnp.float32).reshape(
        height, -1
    )


def project_major(table, weight):
    return (
        jnp.dot(table.reshape(-1, E), weight, preferred_element_type=jnp.float32)
        .astype(jnp.bfloat16)
        .reshape(table.shape)
    )


def split_heads(table):
    return table.reshape(table.shape[0], -1, HEADS, HD)


def feature_major(table):
    return jnp.transpose(table.reshape(table.shape[0], -1, E), (1, 0, 2))


def feature_attention(queries, key_table, value_table):
    height = queries.shape[0]
    scores = jnp.einsum(
        "rqhd,rkhd->rhqk",
        split_heads(queries),
        split_heads(key_table),
        preferred_element_type=jnp.float32,
    ) * HD ** (-0.5)
    row_peak = jnp.max(scores, axis=-1, keepdims=True)
    weights = jnp.exp(scores - row_peak)
    totals = jnp.sum(weights, axis=-1)
    mixture = jnp.einsum(
        "rhqk,rkhd->rqhd",
        weights.astype(jnp.bfloat16),
        split_heads(value_table),
        preferred_element_type=jnp.float32,
    )
    mixture = mixture / jnp.transpose(totals, (0, 2, 1))[..., None]
    return mixture.astype(jnp.bfloat16).reshape(height, -1)


def attend_block(state, queries, key_block, value_block):
    weighted, running, totals = state
    scores = jnp.einsum(
        "fkhd,qfhd->fhkq", key_block, queries, preferred_element_type=jnp.float32
    ) * HD ** (-0.5)
    raised = jnp.maximum(running, jnp.max(scores, axis=-2))
    fading = jnp.exp(running - raised)
    weights = jnp.exp(scores - raised[..., None, :])
    totals = totals * fading + jnp.sum(weights, axis=-2)
    update = jnp.einsum(
        "fhkq,fkhd->qfhd",
        weights.astype(jnp.bfloat16),
        value_block,
        preferred_element_type=jnp.float32,
    )
    weighted = weighted * jnp.transpose(fading, (2, 0, 1))[..., None] + update
    return (weighted, raised, totals)


def absorb(state, queries, key_table, value_table):
    groups = key_table.shape[0]
    length = key_table.shape[1]
    span = 512
    number = length // span

    def advance(index, carried):
        key_block = lax.dynamic_slice_in_dim(key_table, index * span, span, 1).reshape(
            groups, span, HEADS, HD
        )
        value_block = lax.dynamic_slice_in_dim(value_table, index * span, span, 1).reshape(
            groups, span, HEADS, HD
        )
        return attend_block(carried, queries, key_block, value_block)

    return lax.fori_loop(0, number, advance, state)


def start_state(height, groups):
    return (
        jnp.zeros((height, groups, HEADS, HD), jnp.float32),
        jnp.full((groups, HEADS, height), far_below, jnp.float32),
        jnp.zeros((groups, HEADS, height), jnp.float32),
    )


def finish(state):
    weighted, running, totals = state
    return (weighted / jnp.transpose(totals, (2, 0, 1))[..., None]).astype(jnp.bfloat16)


def body(train_cells, test_cells, feat_weights, row_weights, mlp_up, mlp_down):
    train_height = train_cells.shape[0]
    joined = jnp.concatenate([train_cells, test_cells], axis=0)
    height = joined.shape[0]
    width = joined.shape[1]
    groups = width // E
    start_cells = joined.astype(jnp.float32).reshape(height, groups, E)
    normed_one = layer_norm(start_cells).astype(jnp.bfloat16).reshape(height, width)
    feat_query = project(normed_one, feat_weights[0]).astype(jnp.bfloat16)
    feat_key = project(normed_one, feat_weights[1]).astype(jnp.bfloat16)
    feat_value = project(normed_one, feat_weights[2]).astype(jnp.bfloat16)
    all_keys, all_values = (
        lax.all_gather(feat_key, "feat", axis=1, tiled=True),
        lax.all_gather(feat_value, "feat", axis=1, tiled=True),
    )
    feat_mix = feature_attention(feat_query, all_keys, all_values)
    feat_out = project(feat_mix, feat_weights[3]).astype(jnp.bfloat16)
    after_feat = start_cells + feat_out.astype(jnp.float32).reshape(height, groups, E)
    normed_two = layer_norm(after_feat).astype(jnp.bfloat16).reshape(height, width)
    row_query = project(normed_two, row_weights[0]).astype(jnp.bfloat16)
    train_normed = normed_two[:train_height]
    query_heads = split_heads(row_query)
    initial = start_state(height, groups)
    piece = lax.all_gather(feature_major(train_normed), "rows", axis=1, tiled=True)
    piece_keys = project_major(piece, row_weights[1])
    piece_values = project_major(piece, row_weights[2])
    state = absorb(initial, query_heads, piece_keys, piece_values)
    row_mix = finish(state).reshape(height, width)
    after_row = after_feat + project(row_mix, row_weights[3]).reshape(height, groups, E)
    normed_three = layer_norm(after_row).astype(jnp.bfloat16)
    hidden = jax.nn.gelu(
        jnp.dot(normed_three.reshape(-1, E), mlp_up, preferred_element_type=jnp.float32),
        approximate=False,
    ).astype(jnp.bfloat16)
    lowered = jnp.dot(hidden, mlp_down, preferred_element_type=jnp.float32).reshape(
        height, groups, E
    )
    result = (after_row + lowered).astype(jnp.bfloat16).reshape(height, width)
    return (result[:train_height], result[train_height:])


def solution(mesh):
    return jax.shard_map(
        body,
        mesh=mesh,
        in_specs=(P("rows", "feat"), P("rows", "feat"), P(), P(), P(), P()),
        out_specs=(P("rows", "feat"), P("rows", "feat")),
        check_vma=False,
    )
```

profile of v0, /device:TPU:0, one launch (start us, length us, event | category | flops | bytes accessed | tf_op | source)
XLA Modules:
  0.0 117.8 jit_solution(1699699324572972677)
XLA Ops:
  7.2 0.9 concatenate.13
  8.2 1.1 concatenate.12
  11.9 7.5 %all_gather.10 = bf16[96,1536]{1,0:T(8,128)(2,1)S(1)} all-gather(bf16[96,768]{1,0:T(8,128)(2,1)S(1)} %convert_element_type.137), channel_id=1, replica_groups=mesh['rows'=16,'feat'=2] {'feat'}, dimensions={1}, use_global_device_ids=true | all-gather | bytes 442368 | tf_op jit(solution)/shard_map/all_gather | solution.py:127
  19.6 5.8 %all_gather.9 = bf16[96,1536]{1,0:T(8,128)(2,1)S(1)} all-gather(bf16[96,768]{1,0:T(8,128)(2,1)S(1)} %convert_element_type.134), channel_id=1, replica_groups=mesh['rows'=16,'feat'=2] {'feat'}, dimensions={1}, use_global_device_ids=true | all-gather | bytes 442368 | tf_op jit(solution)/shard_map/all_gather | solution.py:128
  27.3 1.8 %copy.83 = bf16[96,8,6,32]{3,1,2,0:T(8,128)(2,1)} copy(bf16[96,8,6,32]{0,3,2,1:T(8,128)(2,1)S(1)} %bitcast.103) | data formatting | bytes 589824 | tf_op jit(solution)/shard_map/reshape | solution.py:37
  30.0 1.0 fusion.113
  31.0 1.6 %fusion.27 = f32[96,6,4]{2,1,0:T(8,128)S(1)} fusion(f32[96,6,4,8]{3,2,1,0:T(4,128)S(1)} %get-tuple-element.204, f32[96,6,4]{2,1,0:T(8,128)S(1)} %get-tuple-element.203), kind=kLoop, calls=%fused_computation.49 | loop fusion | flops 34560 | bytes 92160 | tf_op jit(solution)/shard_map/reduce_sum | solution.py:54
  32.7 1.2 fusion.29
  34.5 1.2 %copy.86 = bf16[96,4,6,32]{3,2,1,0:T(8,128)(2,1)S(1)} copy(bf16[96,4,6,32]{0,3,2,1:T(8,128)(2,1)S(1)} %fusion.62) | data formatting | bytes 294912 | tf_op jit(solution)/shard_map/convert_element_type | solution.py:62
  39.3 0.9 convolution_convert_fusion.2
  40.3 41.8 %all-gather.2.cloned.1.call-done = bf16[4,1024,192]{2,1,0:T(8,128)(2,1)} async-done(((bf16[4,64,192]{2,1,0:T(8,128)(2,1)}), bf16[4,1024,192]{2,1,0:T(8,128)(2,1)}) %all-gather.2.cloned.1.call-update) | async-done | bytes 1572880 | tf_op jit(solution)/shard_map/all_gather | solution.py:138
  82.0 3.7 %convolution_convert_fusion = bf16[4096,192]{0,1:T(8,128)(2,1)} fusion(bf16[4096,192]{1,0:T(8,128)(2,1)} %bitcast.100, bf16[4,192,192]{2,1,0:T(8,128)(2,1)S(1)} %copy-done.10), kind=kOutput, calls=%fused_computation.18 | convolution fusion | flops 302776320 | bytes 3244032 | tf_op jit(solution)/shard_map/dot_general | solution.py:30
  85.8 1.7 %convolution_convert_fusion.1 = bf16[4096,192]{0,1:T(8,128)(2,1)S(1)} fusion(bf16[4096,192]{1,0:T(8,128)(2,1)S(1)} %bitcast.101, bf16[4,192,192]{2,1,0:T(8,128)(2,1)} %param.11), kind=kOutput, calls=%fused_computation.19 | convolution fusion | flops 302776320 | bytes 3244032 | tf_op jit(solution)/shard_map/dot_general | solution.py:30
  87.5 1.2 %reshape.284 = bf16[4,1024,192]{1,0,2:T(4,128)(2,1)S(1)} reshape(bf16[4096,192]{0,1:T(8,128)(2,1)S(1)} %convolution_convert_fusion.1) | data formatting | bytes 3145728 | tf_op jit(solution)/shard_map/reshape | solution.py:32
  88.7 2.9 %reshape.285 = bf16[4,1024,192]{1,0,2:T(4,128)(2,1)S(1)} reshape(bf16[4096,192]{0,1:T(8,128)(2,1)} %convolution_convert_fusion) | data formatting | bytes 3145728 | tf_op jit(solution)/shard_map/reshape | solution.py:32
  91.6 11.2 %while.18 = (s32[]{:T(128)}, f32[96,4,6,32]{0,3,2,1:T(8,128)}, f32[4,6,96]{2,1,0:T(8,128)S(1)}, f32[4,6,96]{2,1,0:T(8,128)S(1)}, bf16[4,1024,192]{1,0,2:T(4,128)...) while((s32[]{:T(128)}, f32[96,4,6,32]{0,3,2,1:T(8,128)}, ...), condition=%wide.region_9.0_spmd.clone, body=%wide.region_6.0_spmd.clone.sunk | while | flops 160667136 | bytes 25854212 | solution.py:99
  93.3 0.9 multiply_reduce_fusion.5
  94.2 1.4 %fusion.145 = f32[96,4,6,32]{0,3,2,1:T(8,128)S(1)} fusion(bf16[4,512,6,32]{1,3,2,0:T(8,128)(2,1)S(1)} %bitcast.98, f32[4,6,512,96]{2,3,1,0:T(8,128)S(1)} %get-tuple-element.259, f32[4,6,96]{2,1,0:T(8,128)S(1)} %get-tuple-element.287, f32[96,4,6,32]{0,3,2,1:T(8,128)S(1)} %copy-done.1, f32[96,4,6]{0,2,1:T(8,128)S(1)} %get-tuple-element.262, ...), kind=kOutput, calls=%fused_computation.8.clone.1 | convolution fusion | flops 79257600 | bytes 6113281 | tf_op jit(solution)/shard_map/while/body/eval_jaxpr/fhkq,fkhd->qfhd/dot_general | solution.py:74
  95.6 1.4 %fusion.146 = f32[4,6,96]{2,1,0:T(8,128)S(1)} fusion(f32[4,6,512,96]{2,3,1,0:T(8,128)S(1)} %get-tuple-element.259, f32[4,6,96]{2,1,0:T(8,128)S(1)} %get-tuple-element.287), kind=kLoop, calls=%fused_computation.2.clone.1 | loop fusion | flops 3536640 | bytes 4737024 | tf_op jit(solution)/shard_map/while/body/eval_jaxpr/reduce_sum | solution.py:73
  99.7 1.4 %fusion.145 = f32[96,4,6,32]{0,3,2,1:T(8,128)S(1)} fusion(bf16[4,512,6,32]{1,3,2,0:T(8,128)(2,1)S(1)} %bitcast.98, f32[4,6,512,96]{2,3,1,0:T(8,128)S(1)} %get-tuple-element.259, f32[4,6,96]{2,1,0:T(8,128)S(1)} %get-tuple-element.287, f32[96,4,6,32]{0,3,2,1:T(8,128)S(1)} %copy-done.1, f32[96,4,6]{0,2,1:T(8,128)S(1)} %get-tuple-element.262, ...), kind=kOutput, calls=%fused_computation.8.clone.1 | convolution fusion | flops 79257600 | bytes 6113281 | tf_op jit(solution)/shard_map/while/body/eval_jaxpr/fhkq,fkhd->qfhd/dot_general | solution.py:74
  101.1 1.4 %fusion.146 = f32[4,6,96]{2,1,0:T(8,128)S(1)} fusion(f32[4,6,512,96]{2,3,1,0:T(8,128)S(1)} %get-tuple-element.259, f32[4,6,96]{2,1,0:T(8,128)S(1)} %get-tuple-element.287), kind=kLoop, calls=%fused_computation.2.clone.1 | loop fusion | flops 3536640 | bytes 4737024 | tf_op jit(solution)/shard_map/while/body/eval_jaxpr/reduce_sum | solution.py:73
  102.8 1.0 divide_convert_fusion
  103.8 1.5 %fusion.114 = (f32[96,4]{0,1:T(4,128)S(1)}, f32[96,4,192]{2,0,1:T(8,128)S(1)}) fusion(f32[96,4,192]{2,0,1:T(8,128)} %copy-done.5, bf16[96,4,192]{0,2,1:T(8,128)(2,1)S(1)} %bitcast.106, bf16[4,192,192]{2,1,0:T(8,128)(2,1)} %param.11), kind=kOutput, calls=%fused_computation.155 | convolution fusion | flops 28458624 | bytes 935424 | tf_op jit(solution)/shard_map/dot_general | solution.py:23
  106.1 3.0 %fusion.25 = f32[384,192]{1,0:T(8,128)S(1)} fusion(bf16[768,192]{0,1:T(8,128)(2,1)S(1)} %copy-done, bf16[384,192]{1,0:T(8,128)(2,1)S(1)} %reshape.286, bf16[192,768]{1,0:T(8,128)(2,1)S(1)} %copy-done.11), kind=kOutput, calls=%fused_computation.42 | convolution fusion | flops 245661696 | bytes 1032192 | tf_op jit(solution)/shard_map/dot_general | solution.py:149
  (112 shorter events, 16.5 us)
Async XLA Ops:
  7.2 98.9 %copy-start = (bf16[768,192]{0,1:T(8,128)(2,1)S(1)}, bf16[768,192]{0,1:T(8,128)(2,1)}, u32[]{:S(2)}) copy-start(bf16[768,192]{0,1:T(8,128)(2,1)} %param.13) | copy-start | bytes 884740
  7.2 74.9 %all-gather.2.cloned.1.call-start = ((), (), s32[]{:S(2)}) async-start(), calls=%async_computation | async-start | bytes 2228224 | tf_op jit(solution)/shard_map/all_gather | solution.py:138
  8.2 2.1 %copy-start.8 = (bf16[4,192,192]{2,1,0:T(8,128)(2,1)S(1)}, bf16[4,192,192]{2,1,0:T(8,128)(2,1)}, u32[]{:S(2)}) copy-start(bf16[4,192,192]{2,1,0:T(8,128)(2,1)} %param.10) | copy-start | bytes 884740
  9.9 0.9 slice-start
  31.0 1.7 %copy-start.6 = (bf16[96,8,6,32]{3,1,2,0:T(8,128)(2,1)S(1)}, bf16[96,8,6,32]{3,1,2,0:T(8,128)(2,1)}, u32[]{:S(2)}) copy-start(bf16[96,8,6,32]{3,1,2,0:T(8,128)(2,1)} %copy.83) | copy-start | bytes 884740
  34.4 1.8 %copy-start.7 = (f32[384,192]{0,1:T(8,128)S(1)}, f32[384,192]{0,1:T(8,128)}, u32[]{:S(2)}) copy-start(f32[384,192]{0,1:T(8,128)} %copy.90) | copy-start | bytes 884740
  34.4 1.8 %copy-start.9 = (bf16[4,192,192]{2,1,0:T(8,128)(2,1)S(1)}, bf16[4,192,192]{2,1,0:T(8,128)(2,1)}, u32[]{:S(2)}) copy-start(bf16[4,192,192]{2,1,0:T(8,128)(2,1)} %param.10) | copy-start | bytes 884740
  37.1 1.8 %copy-start.10 = (bf16[4,192,192]{2,1,0:T(8,128)(2,1)S(1)}, bf16[4,192,192]{2,1,0:T(8,128)(2,1)}, u32[]{:S(2)}) copy-start(bf16[4,192,192]{2,1,0:T(8,128)(2,1)} %param.11) | copy-start | bytes 884740
  37.4 0.7 copy-start.5
  82.0 3.7 %copy-start.3 = (bf16[4,1024,192]{2,1,0:T(8,128)(2,1)S(1)}, bf16[4,1024,192]{2,1,0:T(8,128)(2,1)}, u32[]{:S(2)}) copy-start(bf16[4,1024,192]{2,1,0:T(8,128)(2,1)} %all-gather.2.cloned.1.call-done) | copy-start | bytes 4718596
  92.3 0.9 copy-start.4
  93.3 1.0 copy-start.1
  95.6 1.4 %copy-start.2 = (f32[96,4,6,32]{0,3,2,1:T(8,128)}, f32[96,4,6,32]{0,3,2,1:T(8,128)S(1)}, u32[]{:S(2)}) copy-start(f32[96,4,6,32]{0,3,2,1:T(8,128)S(1)} %fusion.145) | copy-start | bytes 884740 | tf_op jit(solution)/shard_map/while
  97.8 0.9 copy-start.4
  98.7 1.0 copy-start.1
  101.1 1.4 %copy-start.2 = (f32[96,4,6,32]{0,3,2,1:T(8,128)}, f32[96,4,6,32]{0,3,2,1:T(8,128)S(1)}, u32[]{:S(2)}) copy-start(f32[96,4,6,32]{0,3,2,1:T(8,128)S(1)} %fusion.145) | copy-start | bytes 884740 | tf_op jit(solution)/shard_map/while
  103.8 2.2 %copy-start.11 = (bf16[192,768]{1,0:T(8,128)(2,1)S(1)}, bf16[192,768]{1,0:T(8,128)(2,1)}, u32[]{:S(2)}) copy-start(bf16[192,768]{1,0:T(8,128)(2,1)} %param.12) | copy-start | bytes 884740
Sparse Core Ops, SparseCore 0:
  39.0 42.9 all-gather.1
where the time goes:
time: 118 us
  waiting for transfers between devices  41.8 us (35%)
  local copies, waits for them, and re-layouts  21.5 us (18%)
  matrix products  18.4 us (16%)
  between operations  14.6 us (12%)
  blocking collectives  13.3 us (11%)
  other arithmetic  7.71 us (7%)
    all_gather x1, waiting for transfers between devices, body(): lax.all_gather(feature_major(train_normed), 'rows', axis=1, tiled=True)  41.8 us
    all_gather x1, blocking collectives, body(): lax.all_gather(feat_key, 'feat', axis=1, tiled=True)  7.49 us
    all_gather x1, blocking collectives, body(): lax.all_gather(feat_value, 'feat', axis=1, tiled=True)  5.81 us
    dot_general x2, matrix products, project_major(): jnp.dot(table.reshape(-1, E), weight, preferred_element_type=jnp.float32)  5.47 us
    reshape x2, local copies, waits for them, and re-layouts, project_major(): return jnp.dot(table.reshape(-1, E), weight, preferred_element_type=jnp.f...  4.07 us
    dot_general x6, matrix products, project(): jnp.dot(normed.reshape(-1, E), weight, preferred_element_type=jnp.float32)  3.39 us
    dot_general x1, matrix products, body(): jnp.dot(hidden, mlp_down, preferred_element_type=jnp.float32)  2.96 us
    reduce_sum x2, other arithmetic, attend_block(): totals = totals * fading + jnp.sum(weights, axis=-2)  2.8 us
  transfers between devices with their start and end apart: 1, of which 1 were waited for; matrix products, arithmetic and copies ran while one was open for 1% of the time, Pallas kernels for 0%

commit v1 on v0

v1 whole, which is shorter than its diff:
```python
import functools

import jax
import jax.numpy as jnp
from jax import lax
from jax.experimental import pallas as pl
from jax.experimental.pallas import tpu as pltpu
from jax.sharding import PartitionSpec as P

HD = 32
EPS = 1e-05
LOG2E = 1.4426950408889634
MESH = pl.DeviceIdType.MESH
BF = jnp.bfloat16
F32 = jnp.float32


def layer_norm(x):
    centred = x - jnp.mean(x, axis=-1, keepdims=True)
    spread = jnp.mean(centred * centred, axis=-1, keepdims=True)
    return centred * lax.rsqrt(spread + EPS)


def dot(a, b):
    return jnp.dot(a, b, preferred_element_type=F32)


def dot_t(a, b):
    return lax.dot_general(a, b, (((1,), (1,)), ((), ())), preferred_element_type=F32)


def pack(x):
    n = x.shape[0]
    low = jnp.concatenate([x[: n // 2, 128:], x[n // 2 :, 128:]], axis=1)
    return jnp.concatenate([x[:, :128], low], axis=0)


def unpack(p):
    n = p.shape[0] * 2 // 3
    low = p[n:]
    high = jnp.concatenate([low[:, :64], low[:, 64:]], axis=0)
    return jnp.concatenate([p[:n], high], axis=1)


def gelu(x):
    return 0.5 * x * (1.0 + lax.erf(x * (0.5**0.5)))


def kernel(
    rows_n,
    feats_n,
    train_ref,
    test_ref,
    fw_hbm,
    rw_hbm,
    up_hbm,
    down_hbm,
    train_out,
    test_out,
    fw,
    rw,
    up,
    down,
    o_train,
    o_test,
    outbox,
    inbox,
    ring,
    scores,
    values,
    queries,
    back_out,
    back_in,
    w_sem,
    f_send,
    f_recv,
    q_send,
    q_recv,
    r_send,
    r_recv,
    b_send,
    b_recv,
):
    width = fw.shape[-1]
    quad = outbox.shape[0]
    heads = width // HD
    groups_n = rows_n // quad
    half = groups_n // 2
    n_train = train_ref.shape[0]
    n_test = test_ref.shape[0]
    cell_rows = n_train + n_test
    scale = LOG2E * HD ** (-0.5)

    my_row = lax.axis_index("rows")
    my_feat = lax.axis_index("feat")
    member = lax.rem(my_row, quad)
    group = my_row // quad

    def mate(k):
        return group * quad + lax.rem(member + k, quad)

    right = lax.rem(group + 1, groups_n) * quad + member
    left = lax.rem(group + groups_n - 1, groups_n) * quad + member
    other = lax.rem(my_feat + 1, feats_n)

    loads = [
        pltpu.make_async_copy(s, d, w_sem.at[i])
        for i, (s, d) in enumerate([(fw_hbm, fw), (rw_hbm, rw), (up_hbm, up), (down_hbm, down)])
    ]
    for c in loads:
        c.start()

    barrier = pltpu.get_barrier_semaphore()
    pl.semaphore_signal(barrier, inc=1, device_id={"feat": other}, device_id_type=MESH)
    for k in range(1, quad):
        pl.semaphore_signal(barrier, inc=1, device_id={"rows": mate(k)}, device_id_type=MESH)
    for d in (right, left):
        pl.semaphore_signal(barrier, inc=1, device_id={"rows": d}, device_id_type=MESH)
    pl.semaphore_wait(barrier, quad + 2)

    swaps = [
        pltpu.make_async_remote_copy(
            src_ref=s,
            dst_ref=d,
            send_sem=f_send.at[i],
            recv_sem=f_recv.at[i],
            device_id={"feat": other},
            device_id_type=MESH,
        )
        for i, (s, d) in enumerate([(train_ref, o_train), (test_ref, o_test)])
    ]
    for c in swaps:
        c.start()

    def feature_rows(tr, te):
        parts = []
        for f in range(quad):
            sl = slice(f * width, (f + 1) * width)
            parts += [tr[:, sl].astype(F32), te[:, sl].astype(F32)]
        return jnp.concatenate(parts, axis=0)

    def split(x):
        return [x[f * cell_rows : (f + 1) * cell_rows] for f in range(quad)]

    cells = feature_rows(train_ref[...], test_ref[...])
    n_one = layer_norm(cells).astype(BF)
    loads[0].wait()
    q = split((dot(n_one, fw[0]) * scale).astype(BF))
    ks = split(dot(n_one, fw[1]).astype(BF))
    vs = split(dot(n_one, fw[2]).astype(BF))
    for c in swaps:
        c.wait()
    n_two = layer_norm(feature_rows(o_train[...], o_test[...])).astype(BF)
    ks += split(dot(n_two, fw[1]).astype(BF))
    vs += split(dot(n_two, fw[2]).astype(BF))

    same = (
        lax.broadcasted_iota(jnp.int32, (width, width), 0) // HD
        == lax.broadcasted_iota(jnp.int32, (width, width), 1) // HD
    )
    spread = jnp.where(same, 1.0, 0.0).astype(BF)
    mixes = []
    for f in range(quad):
        prod = jnp.concatenate([q[f] * k for k in ks], axis=0)
        s = dot(prod, spread)
        s = [s[g * cell_rows : (g + 1) * cell_rows] for g in range(len(ks))]
        top = functools.reduce(jnp.maximum, s)
        total = None
        mix = None
        for g in range(len(ks)):
            e = jnp.exp2(s[g] - top)
            t = e * vs[g].astype(F32)
            total = e if total is None else total + e
            mix = t if mix is None else mix + t
        mixes.append((mix / total).astype(BF))
    feat_out = dot(jnp.concatenate(mixes, axis=0), fw[3])
    after = split((cells + feat_out).astype(BF))
    for f in range(quad):
        outbox[f] = pack(after[f])

    sends = []
    for k in (2, 3, 1):
        c = pltpu.make_async_remote_copy(
            src_ref=outbox.at[lax.rem(member + k, quad)],
            dst_ref=inbox.at[k],
            send_sem=q_send.at[k],
            recv_sem=q_recv.at[k],
            device_id={"rows": mate(k)},
            device_id_type=MESH,
        )
        c.start()
        sends.append(c)
    inbox[0] = outbox[member]
    for c in sends:
        c.wait()

    after_feat = [unpack(inbox[k]).astype(F32) for k in range(quad)]
    normed = [layer_norm(x).astype(BF) for x in after_feat]
    for p in range(2):
        ring[0, p] = pack(
            jnp.concatenate([normed[2 * p][:n_train], normed[2 * p + 1][:n_train]], axis=0)
        )

    def hop(way, h, p):
        last = h == half - 1
        src = 0 if h == 0 else 2 * h - 1 + way
        dst = 2 * half - 1 if last else 1 + 2 * h + way
        return pltpu.make_async_remote_copy(
            src_ref=ring.at[src, p],
            dst_ref=ring.at[dst, p],
            send_sem=r_send.at[way, h, p],
            recv_sem=r_recv.at[way, h, p],
            device_id={"rows": left if way else right},
            device_id_type=MESH,
        )

    def pieces(way, h):
        return (way,) if h == half - 1 else (way, 1 - way)

    hops = {}
    for way in range(2):
        for p in pieces(way, 0):
            hops[way, 0, p] = hop(way, 0, p)
            hops[way, 0, p].start()

    loads[1].wait()
    n_all = jnp.concatenate(normed, axis=0)
    q_all = (dot(n_all, rw[0]) * scale).astype(BF)
    lane_head = lax.broadcasted_iota(jnp.int32, (1, width), 1) // HD
    for h in range(heads):
        queries[h] = jnp.where(lane_head == h, q_all, jnp.zeros_like(q_all))

    n_query = q_all.shape[0]
    span = 2 * ring.shape[2] * 2 // 3

    def keys_of(slot):
        return jnp.concatenate([unpack(ring[slot, 0]), unpack(ring[slot, 1])], axis=0)

    def take(slot, column):
        x = keys_of(slot)
        key = dot(x, rw[1]).astype(BF)
        value = dot(x, rw[2]).astype(BF)
        rows = slice(column * span, (column + 1) * span)
        values[rows, :width] = value
        for h in range(heads):
            scores[h, :, rows] = dot_t(queries[h], key)

    take(0, 0) if half <= 2 else None
    for h in range(half):
        if h + 1 < half:
            for way in range(2):
                for p in pieces(way, h + 1):
                    hops[way, h, p].wait_recv()
                    hops[way, h + 1, p] = hop(way, h + 1, p)
                    hops[way, h + 1, p].start()
            for way in range(2):
                for p in pieces(way, h):
                    if p not in pieces(way, h + 1):
                        hops[way, h, p].wait_recv()
            if half <= 2:
                take(1 + 2 * h, 1 + 2 * h)
                take(2 + 2 * h, 2 + 2 * h)
        else:
            for way in range(2):
                for p in pieces(way, h):
                    hops[way, h, p].wait_recv()
            if half <= 2:
                take(2 * half - 1, 2 * half - 1)

    values[:, width:] = jnp.ones_like(values[:, width:])

    def attend(h, carried):
        s = scores[h]
        top = jnp.max(s, axis=-1, keepdims=True)
        if carried is not None:
            top = jnp.maximum(top, carried[0])
        e = jnp.exp2(s - top).astype(BF)
        out = dot(e, values[...])
        if carried is not None:
            out = out + carried[1] * jnp.exp2(carried[0] - top)
        return top, out

    if half <= 2:
        states = [attend(h, None) for h in range(heads)]
    else:
        per = scores.shape[2] // span

        def step(i, states):
            for j in range(per):
                take(i * per + j, j)
            return [attend(h, states[h]) for h in range(heads)]

        start = [
            (
                jnp.full((n_query, 1), -1e30, F32),
                jnp.zeros((n_query, values.shape[1]), F32),
            )
            for _ in range(heads)
        ]
        states = lax.fori_loop(0, groups_n // per, step, start)

    mixed = None
    for h in range(heads):
        out = states[h][1]
        part = out[:, :width] * (1.0 / out[:, width : width + 1])
        mixed = part if h == 0 else jnp.where(lane_head == h, part, mixed)
    mixed = mixed.astype(BF)

    for c in loads[2:]:
        c.wait()
    returns = []
    for k in (2, 1, 3, 0):
        rows = slice(k * cell_rows, (k + 1) * cell_rows)
        after_row = after_feat[k] + dot(mixed[rows], rw[3])
        hidden = gelu(dot(layer_norm(after_row).astype(BF), up[...])).astype(BF)
        done = pack((after_row + dot(hidden, down[...])).astype(BF))
        if k == 0:
            back_in[0] = done
            continue
        back_out[k] = done
        c = pltpu.make_async_remote_copy(
            src_ref=back_out.at[k],
            dst_ref=back_in.at[k],
            send_sem=b_send.at[k],
            recv_sem=b_recv.at[k],
            device_id={"rows": mate(quad - k)},
            device_id_type=MESH,
        )
        c.start()
        returns.append(c)
    for c in returns:
        c.wait()
    for c in hops.values():
        c.wait_send()

    outs = [unpack(back_in[lax.rem(f + quad - member, quad)]) for f in range(quad)]
    result = jnp.concatenate(outs, axis=1)
    train_out[...] = result[:n_train]
    test_out[...] = result[n_train:]


def solution(mesh):
    rows_n = mesh.shape["rows"]
    feats_n = mesh.shape["feat"]

    def body(train, test, fw, rw, up, down):
        width = fw.shape[-1]
        quad = train.shape[1] // width
        heads = width // HD
        n_train, n_test = train.shape[0], test.shape[0]
        cell_rows = n_train + n_test
        groups_n = rows_n // quad
        half = groups_n // 2
        span = quad * n_train
        keys = min(groups_n, 4) * span
        packed = cell_rows * width // 128
        vmem = pltpu.VMEM
        dma = pltpu.SemaphoreType.DMA
        vspec = pl.BlockSpec(memory_space=pltpu.VMEM)
        aspec = pl.BlockSpec(memory_space=pl.ANY)
        return pl.pallas_call(
            functools.partial(kernel, rows_n, feats_n),
            out_shape=(
                jax.ShapeDtypeStruct(train.shape, BF),
                jax.ShapeDtypeStruct(test.shape, BF),
            ),
            in_specs=[vspec, vspec, aspec, aspec, aspec, aspec],
            out_specs=(vspec, vspec),
            scratch_shapes=[
                vmem(fw.shape, BF),
                vmem(rw.shape, BF),
                vmem(up.shape, BF),
                vmem(down.shape, BF),
                vmem(train.shape, BF),
                vmem(test.shape, BF),
                vmem((quad, packed, 128), BF),
                vmem((quad, packed, 128), BF),
                vmem((groups_n, 2, span * width // 256, 128), BF),
                vmem((heads, quad * cell_rows, keys), F32),
                vmem((keys, 256), BF),
                vmem((heads, quad * cell_rows, width), BF),
                vmem((quad, packed, 128), BF),
                vmem((quad, packed, 128), BF),
                dma((4,)),
                dma((2,)),
                dma((2,)),
                dma((quad,)),
                dma((quad,)),
                dma((2, half, 2)),
                dma((2, half, 2)),
                dma((quad,)),
                dma((quad,)),
            ],
            compiler_params=pltpu.CompilerParams(
                collective_id=0, has_side_effects=True, vmem_limit_bytes=60 * 1024 * 1024
            ),
            name="layer",
        )(train, test, fw, rw, up, down)

    return jax.shard_map(
        body,
        mesh=mesh,
        in_specs=(P("rows", "feat"), P("rows", "feat"), P(), P(), P(), P()),
        out_specs=(P("rows", "feat"), P("rows", "feat")),
        check_vma=False,
    )
```

time: 118 us -> 37.6 us (0.32)
  waiting for transfers between devices: 41.8 us -> 0 us
  Pallas kernels: 0 us -> 32.7 us
  matrix products: 18.4 us -> 0 us
  local copies, waits for them, and re-layouts: 21.5 us -> 4.05 us
  between operations: 14.6 us -> 0.65 us
  blocking collectives: 13.3 us -> 0 us
  other arithmetic: 7.71 us -> 0 us
    all_gather x1 -> x0, waiting for transfers between devices: 41.8 us -> none  [body(): lax.all_gather(feature_major(train_normed), 'rows', axis=1, tiled=True)]
    pallas_call x0 -> x1, Pallas kernels: none -> 32.7 us  [body(): pl.pallas_call(functools.partial(kernel, rows_n, feats_n), out_shape=(jax...]
    dot_general x15 -> x0, matrix products: 18.4 us -> none  [the longest x2 5.47 us: project_major(): jnp.dot(table.reshape(-1, E), weight, preferred_element_type=jnp.float32)]
    all_gather x2 -> x0, blocking collectives: 13.3 us -> none  [the longest x1 7.49 us: body(): lax.all_gather(feat_key, 'feat', axis=1, tiled=True)]
    reshape x6 -> x0, local copies, waits for them, and re-layouts: 7 us -> none  [the longest x2 4.07 us: project_major(): return jnp.dot(table.reshape(-1, E), weight, preferred_element_type=jnp.f...]
    reduce_sum x7 -> x0, other arithmetic: 5.15 us -> none  [the longest x2 2.8 us: attend_block(): totals = totals * fading + jnp.sum(weights, axis=-2)]
    convert_element_type x15 -> x0, local copies, waits for them, and re-layouts: 4.41 us -> none  [the longest x3 1.26 us: body(): start_cells = joined.astype(jnp.float32).reshape(height, groups, E)]
    unnamed x21 -> x5, local copies, waits for them, and re-layouts: 1.02 us -> 4.05 us
  transfers between devices with their start and end apart: 1 -> 0, of which waited for: 1 -> 0; matrix products, arithmetic and copies ran while one was open for 1% -> 0% of each run, Pallas kernels for 0% -> 0%
where the time goes in v1:
time: 37.6 us; the launch traced here: 37.4 us
  Pallas kernels  32.7 us (87%)
  local copies, waits for them, and re-layouts  4.05 us (11%)
  between operations  0.65 us (2%)
    pallas_call x1, Pallas kernels, body(): pl.pallas_call(functools.partial(kernel, rows_n, feats_n), out_shape=(jax...  32.7 us
    unnamed x5, local copies, waits for them, and re-layouts  4.05 us

profile of v1, /device:TPU:0, one launch (start us, length us, event | category | flops | bytes accessed | tf_op | source)
XLA Modules:
  0.0 37.4 jit_solution(12434479473379345076)
XLA Ops:
  0.6 1.9 %copy.8.down_hbm = bf16[768,192]{1,0:T(8,128)(2,1)} copy(bf16[768,192]{0,1:T(8,128)(2,1)} %param.11) | data formatting | bytes 589824 | tf_op args[5]
  2.5 32.7 %layer.1 = (bf16[64,768]{1,0:T(8,128)(2,1)}, bf16[32,768]{1,0:T(8,128)(2,1)}) custom-call(bf16[64,768]{1,0:T(8,128)(2,1)} %train_ref.1, bf16[32,768]{1,0:T(8,128)(2,1)} %test_ref.1, bf16[4,192,192]{2,1,0:T(8,128)(2,1)} %fw_hbm.1, bf16[4,192,192]{2,1,0:T(8,128)(2,1)} %rw_hbm.1, bf16[192,768]{1,0:T(8,128)(2,1)} %up_hbm.1, bf16[768,192]{1,0:T(8,128)(2,1)} %copy.8.down_hbm), custom_call_target="tpu_custom_call" | custom-call | tf_op jit(solution)/shard_map/layer/pallas_call | solution.py:361
  35.2 0.0 copy-start
  35.2 1.6 %copy.11 = bf16[64,768]{1,0:T(8,128)(2,1)} copy(bf16[64,768]{1,0:T(8,128)(2,1)} %get-tuple-element.4) | data formatting | bytes 196608
  36.8 0.0 copy-done
  36.8 0.6 %copy.12 = bf16[32,768]{1,0:T(8,128)(2,1)} copy(bf16[32,768]{1,0:T(8,128)(2,1)S(1)} %copy-done) | data formatting | bytes 98304
Async XLA Ops:
  35.2 1.6 %copy-start = (bf16[32,768]{1,0:T(8,128)(2,1)S(1)}, bf16[32,768]{1,0:T(8,128)(2,1)}, u32[]{:S(2)}) copy-start(bf16[32,768]{1,0:T(8,128)(2,1)} %get-tuple-element.5) | copy-start | bytes 147460

commit v2 on v1

v2 whole, which is shorter than its diff:
```python
import functools

import jax
import jax.numpy as jnp
from jax import lax
from jax.experimental import pallas as pl
from jax.experimental.pallas import tpu as pltpu
from jax.sharding import PartitionSpec as P

HD = 32
EPS = 1e-05
LOG2E = 1.4426950408889634
MESH = pl.DeviceIdType.MESH
BF = jnp.bfloat16
F32 = jnp.float32


def layer_norm(x):
    centred = x - jnp.mean(x, axis=-1, keepdims=True)
    spread = jnp.mean(centred * centred, axis=-1, keepdims=True)
    return centred * lax.rsqrt(spread + EPS)


def dot(a, b):
    return jnp.dot(a, b, preferred_element_type=F32)


def dot_t(a, b):
    return lax.dot_general(a, b, (((1,), (1,)), ((), ())), preferred_element_type=F32)


def pack(x):
    n = x.shape[0]
    low = jnp.concatenate([x[: n // 2, 128:], x[n // 2 :, 128:]], axis=1)
    return jnp.concatenate([x[:, :128], low], axis=0)


def unpack(p):
    n = p.shape[0] * 2 // 3
    low = p[n:]
    high = jnp.concatenate([low[:, :64], low[:, 64:]], axis=0)
    return jnp.concatenate([p[:n], high], axis=1)


def gelu(x):
    return 0.5 * x * (1.0 + lax.erf(x * (0.5**0.5)))


def kernel(
    rows_n,
    feats_n,
    train_hbm,
    test_hbm,
    fw_hbm,
    rw_hbm,
    up_hbm,
    down_hbm,
    train_out,
    test_out,
    fw,
    rw,
    up,
    down,
    train_ref,
    test_ref,
    o_train,
    o_test,
    outbox,
    inbox,
    t_outbox,
    t_inbox,
    ring,
    scores,
    values,
    queries,
    back_out,
    back_in,
    w_sem,
    f_send,
    f_recv,
    q_send,
    q_recv,
    t_send,
    t_recv,
    r_send,
    r_recv,
    b_send,
    b_recv,
):
    width = fw.shape[-1]
    quad = outbox.shape[0]
    heads = width // HD
    groups_n = rows_n // quad
    half = groups_n // 2
    n_train = train_ref.shape[0]
    n_test = test_ref.shape[0]
    scale = LOG2E * HD ** (-0.5)

    my_row = lax.axis_index("rows")
    my_feat = lax.axis_index("feat")
    member = lax.rem(my_row, quad)
    group = my_row // quad

    def partner(k):
        low, high = lax.rem(member, 2), member // 2
        return (1 - high if k // 2 else high) * 2 + (1 - low if k % 2 else low)

    def mate(k):
        return group * quad + partner(k)

    right = lax.rem(group + 1, groups_n) * quad + member
    left = lax.rem(group + groups_n - 1, groups_n) * quad + member
    other = lax.rem(my_feat + 1, feats_n)

    loads = [
        pltpu.make_async_copy(s, d, w_sem.at[i])
        for i, (s, d) in enumerate(
            [
                (train_hbm, train_ref),
                (fw_hbm, fw),
                (test_hbm, test_ref),
                (rw_hbm, rw),
                (up_hbm, up),
                (down_hbm, down),
            ]
        )
    ]
    for c in loads:
        c.start()

    barrier = pltpu.get_barrier_semaphore()
    pl.semaphore_signal(barrier, inc=1, device_id={"feat": other}, device_id_type=MESH)
    for k in range(1, quad):
        pl.semaphore_signal(barrier, inc=1, device_id={"rows": mate(k)}, device_id_type=MESH)
    for d in (right, left):
        pl.semaphore_signal(barrier, inc=1, device_id={"rows": d}, device_id_type=MESH)
    pl.semaphore_wait(barrier, quad + 2)

    swaps = [
        pltpu.make_async_remote_copy(
            src_ref=s,
            dst_ref=d,
            send_sem=f_send.at[i],
            recv_sem=f_recv.at[i],
            device_id={"feat": other},
            device_id_type=MESH,
        )
        for i, (s, d) in enumerate([(train_hbm, o_train), (test_hbm, o_test)])
    ]
    for c in swaps:
        c.start()

    def feature_rows(table):
        return jnp.concatenate(
            [table[:, f * width : (f + 1) * width].astype(F32) for f in range(quad)], axis=0
        )

    def split(x):
        n = x.shape[0] // quad
        return [x[f * n : (f + 1) * n] for f in range(quad)]

    def key_value(normed):
        return split(dot(normed, fw[1]).astype(BF)), split(dot(normed, fw[2]).astype(BF))

    same = (
        lax.broadcasted_iota(jnp.int32, (width, width), 0) // HD
        == lax.broadcasted_iota(jnp.int32, (width, width), 1) // HD
    )
    spread = jnp.where(same, 1.0, 0.0).astype(BF)

    def own_side(table):
        cells = feature_rows(table)
        normed = layer_norm(cells).astype(BF)
        q = split((dot(normed, fw[0]) * scale).astype(BF))
        ks, vs = key_value(normed)
        return cells, q, ks, vs

    def feature_attention(own, table):
        cells, q, ks, vs = own
        n = table.shape[0]
        more_k, more_v = key_value(layer_norm(feature_rows(table)).astype(BF))
        ks, vs = ks + more_k, vs + more_v
        mixes = []
        for f in range(quad):
            prod = jnp.concatenate([q[f] * k for k in ks], axis=0)
            s = dot(prod, spread)
            s = [s[g * n : (g + 1) * n] for g in range(len(ks))]
            top = functools.reduce(jnp.maximum, s)
            total = None
            mix = None
            for g in range(len(ks)):
                e = jnp.exp2(s[g] - top)
                t = e * vs[g].astype(F32)
                total = e if total is None else total + e
                mix = t if mix is None else mix + t
            mixes.append((mix / total).astype(BF))
        feat_out = dot(jnp.concatenate(mixes, axis=0), fw[3])
        return split((cells + feat_out).astype(BF))

    def to_mates(box, landing, send, recv):
        copies = {}
        for k in (2, 3, 1):
            copies[k] = pltpu.make_async_remote_copy(
                src_ref=box.at[partner(k)],
                dst_ref=landing.at[k],
                send_sem=send.at[k],
                recv_sem=recv.at[k],
                device_id={"rows": mate(k)},
                device_id_type=MESH,
            )
            copies[k].start()
        landing[0] = box[member]
        return copies

    loads[0].wait()
    loads[1].wait()
    own = own_side(train_ref[...])
    loads[2].wait()
    own_test = own_side(test_ref[...])
    swaps[0].wait()
    for f, x in enumerate(feature_attention(own, o_train[...])):
        outbox[f] = pack(x)
    moved = to_mates(outbox, inbox, q_send, q_recv)

    def hop(way, h, p):
        last = h == half - 1
        src = 0 if h == 0 else 2 * h - 1 + way
        dst = 2 * half - 1 if last else 1 + 2 * h + way
        return pltpu.make_async_remote_copy(
            src_ref=ring.at[src, p],
            dst_ref=ring.at[dst, p],
            send_sem=r_send.at[way, h, p],
            recv_sem=r_recv.at[way, h, p],
            device_id={"rows": left if way else right},
            device_id_type=MESH,
        )

    def pieces(way, h):
        return (way,) if h == half - 1 else (way, 1 - way)

    hops = {}
    after_train = []
    normed_train = []
    for p in range(2):
        for k in (2 * p, 2 * p + 1):
            if k:
                moved[k].wait_recv()
            after_train.append(unpack(inbox[k]).astype(F32))
            normed_train.append(layer_norm(after_train[k]).astype(BF))
        ring[0, p] = pack(jnp.concatenate(normed_train[2 * p :], axis=0))
        for way in (p, 1 - p):
            if p in pieces(way, 0):
                hops[way, 0, p] = hop(way, 0, p)
                hops[way, 0, p].start()

    swaps[1].wait()
    for f, x in enumerate(feature_attention(own_test, o_test[...])):
        t_outbox[f] = pack(x)
    t_moved = to_mates(t_outbox, t_inbox, t_send, t_recv)

    loads[3].wait()
    lane_head = lax.broadcasted_iota(jnp.int32, (1, width), 1) // HD
    train_rows = slice(0, quad * n_train)
    test_rows = slice(quad * n_train, quad * (n_train + n_test))
    all_rows = slice(0, quad * (n_train + n_test))
    n_query = all_rows.stop
    span = quad * n_train
    values[:, width:] = jnp.ones_like(values[:, width:])

    def ask(normed, rows):
        q_all = (dot(jnp.concatenate(normed, axis=0), rw[0]) * scale).astype(BF)
        for h in range(heads):
            queries[h, rows] = jnp.where(lane_head == h, q_all, jnp.zeros_like(q_all))

    def take(slot, column):
        x = jnp.concatenate([unpack(ring[slot, 0]), unpack(ring[slot, 1])], axis=0)
        values[column * span : (column + 1) * span, :width] = dot(x, rw[2]).astype(BF)
        return dot(x, rw[1]).astype(BF)

    def score(key, column, rows):
        for h in range(heads):
            scores[h, rows, column * span : (column + 1) * span] = dot_t(queries[h, rows], key)

    def attend(h, columns, carried):
        s = scores[h, :, columns]
        top = jnp.max(s, axis=-1, keepdims=True)
        if carried is not None:
            top = jnp.maximum(top, carried[0])
        e = jnp.exp2(s - top).astype(BF)
        out = dot(e, values[columns])
        if carried is not None:
            out = out + carried[1] * jnp.exp2(carried[0] - top)
        return top, out

    ask(normed_train, train_rows)
    if half <= 2:
        own_key = take(0, 0)
        score(own_key, 0, train_rows)

    for h in range(half - 1):
        for way in range(2):
            for p in pieces(way, h + 1):
                hops[way, h, p].wait_recv()
                hops[way, h + 1, p] = hop(way, h + 1, p)
                hops[way, h + 1, p].start()
        for way in range(2):
            for p in pieces(way, h):
                if p not in pieces(way, h + 1):
                    hops[way, h, p].wait_recv()

    after_test = []
    normed_test = []
    for k in range(quad):
        if k:
            t_moved[k].wait_recv()
        after_test.append(unpack(t_inbox[k]).astype(F32))
        normed_test.append(layer_norm(after_test[k]).astype(BF))
    ask(normed_test, test_rows)

    if half <= 2:
        score(own_key, 0, test_rows)
        for slot in range(1, 2 * half - 1):
            score(take(slot, slot), slot, all_rows)
        last = 2 * half - 1
        states = [attend(h, slice(0, last * span), None) for h in range(heads)]

    for way in range(2):
        for p in pieces(way, half - 1):
            hops[way, half - 1, p].wait_recv()

    if half <= 2:
        score(take(last, last), last, all_rows)
        columns = slice(last * span, (last + 1) * span)
        states = [attend(h, columns, states[h]) for h in range(heads)]
    else:
        per = scores.shape[2] // span

        def step(i, states):
            for j in range(per):
                score(take(i * per + j, j), j, all_rows)
            return [attend(h, slice(0, per * span), states[h]) for h in range(heads)]

        start = [
            (
                jnp.full((n_query, 1), -1e30, F32),
                jnp.zeros((n_query, values.shape[1]), F32),
            )
            for _ in range(heads)
        ]
        states = lax.fori_loop(0, groups_n // per, step, start)

    mixed = None
    for h in range(heads):
        out = states[h][1]
        part = out[:, :width] * (1.0 / out[:, width : width + 1])
        mixed = part if h == 0 else jnp.where(lane_head == h, part, mixed)
    mixed = mixed.astype(BF)

    for c in loads[4:]:
        c.wait()
    returns = []
    for pair in ((2, 3), (1, 0)):
        before, picked = [], []
        for k in pair:
            before += [after_train[k], after_test[k]]
            base = test_rows.start + k * n_test
            picked += [mixed[k * n_train : (k + 1) * n_train], mixed[base : base + n_test]]
        after_row = jnp.concatenate(before, axis=0) + dot(jnp.concatenate(picked, axis=0), rw[3])
        hidden = gelu(dot(layer_norm(after_row).astype(BF), up[...])).astype(BF)
        done = (after_row + dot_t(hidden, down[...])).astype(BF)
        for i, k in enumerate(pair):
            n = n_train + n_test
            block = pack(done[i * n : (i + 1) * n])
            if k == 0:
                back_in[0] = block
                continue
            back_out[k] = block
            c = pltpu.make_async_remote_copy(
                src_ref=back_out.at[k],
                dst_ref=back_in.at[k],
                send_sem=b_send.at[k],
                recv_sem=b_recv.at[k],
                device_id={"rows": mate(k)},
                device_id_type=MESH,
            )
            c.start()
            returns.append(c)
    for c in returns:
        c.wait()
    for c in [*hops.values(), *moved.values(), *t_moved.values()]:
        c.wait_send()

    outs = [unpack(back_in[partner(f)]) for f in range(quad)]
    result = jnp.concatenate(outs, axis=1)
    train_out[...] = result[:n_train]
    test_out[...] = result[n_train:]


def solution(mesh):
    rows_n = mesh.shape["rows"]
    feats_n = mesh.shape["feat"]

    def body(train, test, fw, rw, up, down):
        width = fw.shape[-1]
        quad = train.shape[1] // width
        heads = width // HD
        n_train, n_test = train.shape[0], test.shape[0]
        cell_rows = n_train + n_test
        groups_n = rows_n // quad
        half = groups_n // 2
        span = quad * n_train
        keys = min(groups_n, 4) * span
        packed = cell_rows * width // 128
        vmem = pltpu.VMEM
        dma = pltpu.SemaphoreType.DMA
        vspec = pl.BlockSpec(memory_space=pltpu.VMEM)
        aspec = pl.BlockSpec(memory_space=pl.ANY)
        return pl.pallas_call(
            functools.partial(kernel, rows_n, feats_n),
            out_shape=(
                jax.ShapeDtypeStruct(train.shape, BF),
                jax.ShapeDtypeStruct(test.shape, BF),
            ),
            in_specs=[aspec, aspec, aspec, aspec, aspec, aspec],
            out_specs=(vspec, vspec),
            scratch_shapes=[
                vmem(fw.shape, BF),
                vmem(rw.shape, BF),
                vmem(up.shape, BF),
                vmem(down.shape[::-1], BF),
                vmem(train.shape, BF),
                vmem(test.shape, BF),
                vmem(train.shape, BF),
                vmem(test.shape, BF),
                vmem((quad, n_train * width // 128, 128), BF),
                vmem((quad, n_train * width // 128, 128), BF),
                vmem((quad, n_test * width // 128, 128), BF),
                vmem((quad, n_test * width // 128, 128), BF),
                vmem((groups_n, 2, span * width // 256, 128), BF),
                vmem((heads, quad * cell_rows, keys), F32),
                vmem((keys, 256), BF),
                vmem((heads, quad * cell_rows, width), BF),
                vmem((quad, packed, 128), BF),
                vmem((quad, packed, 128), BF),
                dma((6,)),
                dma((2,)),
                dma((2,)),
                dma((quad,)),
                dma((quad,)),
                dma((quad,)),
                dma((quad,)),
                dma((2, half, 2)),
                dma((2, half, 2)),
                dma((quad,)),
                dma((quad,)),
            ],
            compiler_params=pltpu.CompilerParams(
                collective_id=0, has_side_effects=True, vmem_limit_bytes=60 * 1024 * 1024
            ),
            name="layer",
        )(train, test, fw, rw, up, down.T)

    return jax.shard_map(
        body,
        mesh=mesh,
        in_specs=(P("rows", "feat"), P("rows", "feat"), P(), P(), P(), P()),
        out_specs=(P("rows", "feat"), P("rows", "feat")),
        check_vma=False,
    )
```

time: 37.6 us -> 33.5 us (0.89)
  Pallas kernels: 32.7 us -> 30.6 us
  local copies, waits for them, and re-layouts: 4.05 us -> 2.18 us
    pallas_call x1, Pallas kernels: 32.7 us -> 30.6 us  [body(): pl.pallas_call(functools.partial(kernel, rows_n, feats_n), out_shape=(jax...]
    unnamed x5 -> x4, local copies, waits for them, and re-layouts: 4.05 us -> 2.18 us
where the time goes in v2:
time: 33.5 us; the launch traced here: 33.4 us
  Pallas kernels  30.6 us (91%)
  local copies, waits for them, and re-layouts  2.18 us (7%)
  between operations  0.65 us (2%)
    pallas_call x1, Pallas kernels, body(): pl.pallas_call(functools.partial(kernel, rows_n, feats_n), out_shape=(jax...  30.6 us
    unnamed x4, local copies, waits for them, and re-layouts  2.18 us

profile of v2, /device:TPU:0, one launch (start us, length us, event | category | flops | bytes accessed | tf_op | source)
XLA Modules:
  0.0 33.4 jit_solution(9475493707942505786)
XLA Ops:
  0.6 30.6 %layer.1 = (bf16[64,768]{1,0:T(8,128)(2,1)}, bf16[32,768]{1,0:T(8,128)(2,1)}) custom-call(bf16[64,768]{1,0:T(8,128)(2,1)} %train_hbm.1, bf16[32,768]{1,0:T(8,128)(2,1)} %test_hbm.1, bf16[4,192,192]{2,1,0:T(8,128)(2,1)} %fw_hbm.1, bf16[4,192,192]{2,1,0:T(8,128)(2,1)} %rw_hbm.1, bf16[192,768]{1,0:T(8,128)(2,1)} %up_hbm.1, bf16[192,768]{1,0:T(8,128)(2,1)} %bitcast.1), custom_call_target="tpu_custom_call" | custom-call | tf_op jit(solution)/shard_map/layer/pallas_call | solution.py:418
  31.2 0.0 copy-start
  31.2 1.6 %copy.10 = bf16[64,768]{1,0:T(8,128)(2,1)} copy(bf16[64,768]{1,0:T(8,128)(2,1)} %get-tuple-element.4) | data formatting | bytes 196608
  32.8 0.0 copy-done
  32.8 0.6 %copy.11 = bf16[32,768]{1,0:T(8,128)(2,1)} copy(bf16[32,768]{1,0:T(8,128)(2,1)S(1)} %copy-done) | data formatting | bytes 98304
Async XLA Ops:
  31.2 1.6 %copy-start = (bf16[32,768]{1,0:T(8,128)(2,1)S(1)}, bf16[32,768]{1,0:T(8,128)(2,1)}, u32[]{:S(2)}) copy-start(bf16[32,768]{1,0:T(8,128)(2,1)} %get-tuple-element.5) | copy-start | bytes 147460

commit v3 on v2

--- a/solution.py
+++ b/solution.py
@@ -55,8 +55,7 @@
     rw_hbm,
     up_hbm,
     down_hbm,
-    train_out,
-    test_out,
+    back_in,
     fw,
     rw,
     up,
@@ -74,26 +73,24 @@
     values,
     queries,
     back_out,
-    back_in,
     w_sem,
     f_send,
     f_recv,
     q_send,
     q_recv,
-    t_send,
-    t_recv,
     r_send,
     r_recv,
     b_send,
     b_recv,
 ):
     width = fw.shape[-1]
-    quad = outbox.shape[0]
+    quad = t_outbox.shape[0]
     heads = width // HD
     groups_n = rows_n // quad
     half = groups_n // 2
     n_train = train_ref.shape[0]
     n_test = test_ref.shape[0]
+    n_half = n_train // 2
     scale = LOG2E * HD ** (-0.5)
 
     my_row = lax.axis_index("rows")
@@ -136,6 +133,7 @@
         pl.semaphore_signal(barrier, inc=1, device_id={"rows": d}, device_id_type=MESH)
     pl.semaphore_wait(barrier, quad + 2)
 
+    halves = [pl.ds(p * n_half, n_half) for p in range(2)]
     swaps = [
         pltpu.make_async_remote_copy(
             src_ref=s,
@@ -145,7 +143,9 @@
             device_id={"feat": other},
             device_id_type=MESH,
         )
-        for i, (s, d) in enumerate([(train_hbm, o_train), (test_hbm, o_test)])
+        for i, (s, d) in enumerate(
+            [(train_hbm.at[r], o_train.at[r]) for r in halves] + [(test_hbm, o_test)]
+        )
     ]
     for c in swaps:
         c.start()
@@ -197,14 +197,14 @@
         feat_out = dot(jnp.concatenate(mixes, axis=0), fw[3])
         return split((cells + feat_out).astype(BF))
 
-    def to_mates(box, landing, send, recv):
+    def to_mates(box, landing, stage):
         copies = {}
         for k in (2, 3, 1):
             copies[k] = pltpu.make_async_remote_copy(
                 src_ref=box.at[partner(k)],
                 dst_ref=landing.at[k],
-                send_sem=send.at[k],
-                recv_sem=recv.at[k],
+                send_sem=q_send.at[stage, k],
+                recv_sem=q_recv.at[stage, k],
                 device_id={"rows": mate(k)},
                 device_id_type=MESH,
             )
@@ -214,13 +214,20 @@
 
     loads[0].wait()
     loads[1].wait()
-    own = own_side(train_ref[...])
+    own = [own_side(train_ref[p * n_half : (p + 1) * n_half]) for p in range(2)]
+    moved = []
+    boxes = [(outbox.at[p], inbox.at[p]) for p in range(2)] + [(t_outbox, t_inbox)]
+    for p in range(2):
+        swaps[p].wait()
+        for f, x in enumerate(feature_attention(own[p], o_train[p * n_half : (p + 1) * n_half])):
+            outbox[p, f] = pack(x)
+        moved.append(to_mates(*boxes[p], p))
     loads[2].wait()
     own_test = own_side(test_ref[...])
-    swaps[0].wait()
-    for f, x in enumerate(feature_attention(own, o_train[...])):
-        outbox[f] = pack(x)
-    moved = to_mates(outbox, inbox, q_send, q_recv)
+    swaps[2].wait()
+    for f, x in enumerate(feature_attention(own_test, o_test[...])):
+        t_outbox[f] = pack(x)
+    moved.append(to_mates(*boxes[2], 2))
 
     def hop(way, h, p):
         last = h == half - 1
@@ -239,38 +246,46 @@
         return (way,) if h == half - 1 else (way, 1 - way)
 
     hops = {}
-    after_train = []
-    normed_train = []
+    after = []
+    normed = []
+
+    def arrive(stage):
+        for k in range(1, quad):
+            moved[stage][k].wait_recv()
+        landing = boxes[stage][1]
+        after.append(
+            jnp.concatenate([unpack(landing[k]) for k in range(quad)], axis=0).astype(F32)
+        )
+        normed.append(layer_norm(after[stage]).astype(BF))
+
     for p in range(2):
-        for k in (2 * p, 2 * p + 1):
-            if k:
-                moved[k].wait_recv()
-            after_train.append(unpack(inbox[k]).astype(F32))
-            normed_train.append(layer_norm(after_train[k]).astype(BF))
-        ring[0, p] = pack(jnp.concatenate(normed_train[2 * p :], axis=0))
+        arrive(p)
+        ring[0, p] = pack(normed[p])
         for way in (p, 1 - p):
             if p in pieces(way, 0):
                 hops[way, 0, p] = hop(way, 0, p)
                 hops[way, 0, p].start()
 
-    swaps[1].wait()
-    for f, x in enumerate(feature_attention(own_test, o_test[...])):
-        t_outbox[f] = pack(x)
-    t_moved = to_mates(t_outbox, t_inbox, t_send, t_recv)
-
     loads[3].wait()
     lane_head = lax.broadcasted_iota(jnp.int32, (1, width), 1) // HD
-    train_rows = slice(0, quad * n_train)
-    test_rows = slice(quad * n_train, quad * (n_train + n_test))
-    all_rows = slice(0, quad * (n_train + n_test))
-    n_query = all_rows.stop
+    n_query = quad * (n_train + n_test)
+    n_side = n_query // 2
+    sizes = [2 * n_half, 2 * n_half, 2 * n_test]
+    begins = [0, 2 * n_half, 4 * n_half]
+    all_rows = [slice(0, n_query)]
+    train_rows = [slice(i * n_side, i * n_side + begins[2]) for i in range(2)]
+    test_rows = [slice(i * n_side + begins[2], (i + 1) * n_side) for i in range(2)]
     span = quad * n_train
     values[:, width:] = jnp.ones_like(values[:, width:])
 
-    def ask(normed, rows):
-        q_all = (dot(jnp.concatenate(normed, axis=0), rw[0]) * scale).astype(BF)
+    def ask(stage):
+        q_all = (dot(normed[stage], rw[0]) * scale).astype(BF)
+        n = sizes[stage]
         for h in range(heads):
-            queries[h, rows] = jnp.where(lane_head == h, q_all, jnp.zeros_like(q_all))
+            one = jnp.where(lane_head == h, q_all, jnp.zeros_like(q_all))
+            for i in range(2):
+                at = i * n_side + begins[stage]
+                queries[h, at : at + n] = one[(1 - i) * n : (2 - i) * n]
 
     def take(slot, column):
         x = jnp.concatenate([unpack(ring[slot, 0]), unpack(ring[slot, 1])], axis=0)
@@ -279,10 +294,11 @@
 
     def score(key, column, rows):
         for h in range(heads):
-            scores[h, rows, column * span : (column + 1) * span] = dot_t(queries[h, rows], key)
-
-    def attend(h, columns, carried):
-        s = scores[h, :, columns]
+            for r in rows:
+                scores[h, r, column * span : (column + 1) * span] = dot_t(queries[h, r], key)
+
+    def attend(h, rows, columns, carried):
+        s = scores[h, rows, columns]
         top = jnp.max(s, axis=-1, keepdims=True)
         if carried is not None:
             top = jnp.maximum(top, carried[0])
@@ -292,10 +308,17 @@
             out = out + carried[1] * jnp.exp2(carried[0] - top)
         return top, out
 
-    ask(normed_train, train_rows)
+    ask(0)
+    ask(1)
+    everything = slice(0, n_query)
     if half <= 2:
         own_key = take(0, 0)
         score(own_key, 0, train_rows)
+    arrive(2)
+    ask(2)
+    if half <= 2:
+        score(own_key, 0, test_rows)
+        states = [attend(h, everything, slice(0, span), None) for h in range(heads)]
 
     for h in range(half - 1):
         for way in range(2):
@@ -308,37 +331,28 @@
                 if p not in pieces(way, h + 1):
                     hops[way, h, p].wait_recv()
 
-    after_test = []
-    normed_test = []
-    for k in range(quad):
-        if k:
-            t_moved[k].wait_recv()
-        after_test.append(unpack(t_inbox[k]).astype(F32))
-        normed_test.append(layer_norm(after_test[k]).astype(BF))
-    ask(normed_test, test_rows)
-
-    if half <= 2:
-        score(own_key, 0, test_rows)
-        for slot in range(1, 2 * half - 1):
+    if half == 2:
+        for slot in (1, 2):
             score(take(slot, slot), slot, all_rows)
-        last = 2 * half - 1
-        states = [attend(h, slice(0, last * span), None) for h in range(heads)]
+        states = [
+            attend(h, everything, slice(span, 3 * span), states[h]) for h in range(heads)
+        ]
 
     for way in range(2):
         for p in pieces(way, half - 1):
             hops[way, half - 1, p].wait_recv()
 
     if half <= 2:
-        score(take(last, last), last, all_rows)
+        last = 2 * half - 1
+        last_key = take(last, last)
         columns = slice(last * span, (last + 1) * span)
-        states = [attend(h, columns, states[h]) for h in range(heads)]
     else:
         per = scores.shape[2] // span
 
         def step(i, states):
             for j in range(per):
                 score(take(i * per + j, j), j, all_rows)
-            return [attend(h, slice(0, per * span), states[h]) for h in range(heads)]
+            return [attend(h, everything, slice(0, per * span), states[h]) for h in range(heads)]
 
         start = [
             (
@@ -349,35 +363,43 @@
         ]
         states = lax.fori_loop(0, groups_n // per, step, start)
 
-    mixed = None
-    for h in range(heads):
-        out = states[h][1]
-        part = out[:, :width] * (1.0 / out[:, width : width + 1])
-        mixed = part if h == 0 else jnp.where(lane_head == h, part, mixed)
-    mixed = mixed.astype(BF)
-
     for c in loads[4:]:
         c.wait()
     returns = []
-    for pair in ((2, 3), (1, 0)):
-        before, picked = [], []
-        for k in pair:
-            before += [after_train[k], after_test[k]]
-            base = test_rows.start + k * n_test
-            picked += [mixed[k * n_train : (k + 1) * n_train], mixed[base : base + n_test]]
-        after_row = jnp.concatenate(before, axis=0) + dot(jnp.concatenate(picked, axis=0), rw[3])
+    for i, pair in enumerate(((2, 3), (0, 1))):
+        rows = slice(i * n_side, (i + 1) * n_side)
+        side = [tuple(x[rows] for x in states[h]) for h in range(heads)]
+        if half <= 2:
+            score(last_key, last, [rows])
+            side = [attend(h, rows, columns, side[h]) for h in range(heads)]
+        mixed = None
+        for h in range(heads):
+            out = side[h][1]
+            part = out[:, :width] * (1.0 / out[:, width : width + 1])
+            mixed = part if h == 0 else jnp.where(lane_head == h, part, mixed)
+        before = [x[(1 - i) * n : (2 - i) * n] for x, n in zip(after, sizes)]
+        after_row = jnp.concatenate(before, axis=0) + dot(mixed.astype(BF), rw[3])
         hidden = gelu(dot(layer_norm(after_row).astype(BF), up[...])).astype(BF)
         done = (after_row + dot_t(hidden, down[...])).astype(BF)
-        for i, k in enumerate(pair):
-            n = n_train + n_test
-            block = pack(done[i * n : (i + 1) * n])
+        for j, k in enumerate(pair):
+            block = pack(
+                jnp.concatenate(
+                    [
+                        done[b + j * (n // 2) : b + (j + 1) * (n // 2)]
+                        for b, n in zip(begins, sizes)
+                    ],
+                    axis=0,
+                )
+            )
+            back_out[k] = block
             if k == 0:
-                back_in[0] = block
+                c = pltpu.make_async_copy(back_out.at[0], back_in.at[member], b_send.at[0])
+                c.start()
+                returns.append(c)
                 continue
-            back_out[k] = block
             c = pltpu.make_async_remote_copy(
                 src_ref=back_out.at[k],
-                dst_ref=back_in.at[k],
+                dst_ref=back_in.at[member],
                 send_sem=b_send.at[k],
                 recv_sem=b_recv.at[k],
                 device_id={"rows": mate(k)},
@@ -387,11 +409,14 @@
             returns.append(c)
     for c in returns:
         c.wait()
-    for c in [*hops.values(), *moved.values(), *t_moved.values()]:
+    for c in [*hops.values(), *(c for m in moved for c in m.values())]:
         c.wait_send()
 
-    outs = [unpack(back_in[partner(f)]) for f in range(quad)]
-    result = jnp.concatenate(outs, axis=1)
+
+def place(back_ref, train_out, test_out):
+    quad = back_ref.shape[0]
+    result = jnp.concatenate([unpack(back_ref[f]) for f in range(quad)], axis=1)
+    n_train = train_out.shape[0]
     train_out[...] = result[:n_train]
     test_out[...] = result[n_train:]
 
@@ -415,14 +440,11 @@
         dma = pltpu.SemaphoreType.DMA
         vspec = pl.BlockSpec(memory_space=pltpu.VMEM)
         aspec = pl.BlockSpec(memory_space=pl.ANY)
-        return pl.pallas_call(
+        back = pl.pallas_call(
             functools.partial(kernel, rows_n, feats_n),
-            out_shape=(
-                jax.ShapeDtypeStruct(train.shape, BF),
-                jax.ShapeDtypeStruct(test.shape, BF),
-            ),
+            out_shape=jax.ShapeDtypeStruct((quad, packed, 128), BF),
             in_specs=[aspec, aspec, aspec, aspec, aspec, aspec],
-            out_specs=(vspec, vspec),
+            out_specs=aspec,
             scratch_shapes=[
                 vmem(fw.shape, BF),
                 vmem(rw.shape, BF),
@@ -432,8 +454,8 @@
                 vmem(test.shape, BF),
                 vmem(train.shape, BF),
                 vmem(test.shape, BF),
-                vmem((quad, n_train * width // 128, 128), BF),
-                vmem((quad, n_train * width // 128, 128), BF),
+                vmem((2, quad, n_train * width // 256, 128), BF),
+                vmem((2, quad, n_train * width // 256, 128), BF),
                 vmem((quad, n_test * width // 128, 128), BF),
                 vmem((quad, n_test * width // 128, 128), BF),
                 vmem((groups_n, 2, span * width // 256, 128), BF),
@@ -441,14 +463,11 @@
                 vmem((keys, 256), BF),
                 vmem((heads, quad * cell_rows, width), BF),
                 vmem((quad, packed, 128), BF),
-                vmem((quad, packed, 128), BF),
                 dma((6,)),
-                dma((2,)),
-                dma((2,)),
-                dma((quad,)),
-                dma((quad,)),
-                dma((quad,)),
-                dma((quad,)),
+                dma((3,)),
+                dma((3,)),
+                dma((3, quad)),
+                dma((3, quad)),
                 dma((2, half, 2)),
                 dma((2, half, 2)),
                 dma((quad,)),
@@ -459,6 +478,16 @@
             ),
             name="layer",
         )(train, test, fw, rw, up, down.T)
+        return pl.pallas_call(
+            place,
+            out_shape=(
+                jax.ShapeDtypeStruct(train.shape, BF),
+                jax.ShapeDtypeStruct(test.shape, BF),
+            ),
+            in_specs=[vspec],
+            out_specs=(vspec, vspec),
+            name="place",
+        )(back)
 
     return jax.shard_map(
         body,

time: 33.5 us -> 30.8 us (0.919)
  local copies, waits for them, and re-layouts: 2.18 us -> 0 us
  Pallas kernels: 30.6 us -> 30 us
    unnamed x4 -> x0, local copies, waits for them, and re-layouts: 2.18 us -> none
    pallas_call x1 -> x2, Pallas kernels: 30.6 us -> 30 us  [the longest x1 28.3 us: body(): pl.pallas_call(functools.partial(kernel, rows_n, feats_n), out_shape=jax....]
where the time goes in v3:
time: 30.8 us; the launch traced here: 30.7 us
  Pallas kernels  30 us (97%)
  between operations  0.64 us (2%)
    pallas_call x1, Pallas kernels, body(): pl.pallas_call(functools.partial(kernel, rows_n, feats_n), out_shape=jax....  28.3 us
    pallas_call x1, Pallas kernels, body(): pl.pallas_call(place, out_shape=(jax.ShapeDtypeStruct(train.shape, BF), j...  1.7 us

profile of v3, /device:TPU:0, one launch (start us, length us, event | category | flops | bytes accessed | tf_op | source)
XLA Modules:
  0.0 30.7 jit_solution(11456861840463550531)
XLA Ops:
  0.6 28.3 %layer.1.back_ref = bf16[4,144,128]{2,1,0:T(8,128)(2,1)} custom-call(bf16[64,768]{1,0:T(8,128)(2,1)} %train_hbm.1, bf16[32,768]{1,0:T(8,128)(2,1)} %test_hbm.1, bf16[4,192,192]{2,1,0:T(8,128)(2,1)} %fw_hbm.1, bf16[4,192,192]{2,1,0:T(8,128)(2,1)} %rw_hbm.1, bf16[192,768]{1,0:T(8,128)(2,1)} %up_hbm.1, bf16[192,768]{1,0:T(8,128)(2,1)} %bitcast.1), custom_call_target="tpu_custom_call" | custom-call | tf_op jit(solution)/shard_map/layer/pallas_call | solution.py:443
  28.9 1.7 %place.1 = (bf16[64,768]{1,0:T(8,128)(2,1)}, bf16[32,768]{1,0:T(8,128)(2,1)}) custom-call(bf16[4,144,128]{2,1,0:T(8,128)(2,1)} %layer.1.back_ref), custom_call_target="tpu_custom_call" | custom-call | tf_op jit(solution)/shard_map/place/pallas_call | solution.py:481

commit v4 on v3

--- a/solution.py
+++ b/solution.py
@@ -442,9 +442,9 @@
         aspec = pl.BlockSpec(memory_space=pl.ANY)
         back = pl.pallas_call(
             functools.partial(kernel, rows_n, feats_n),
-            out_shape=jax.ShapeDtypeStruct((quad, packed, 128), BF),
+            out_shape=pltpu.VMEM((quad, packed, 128), BF),
             in_specs=[aspec, aspec, aspec, aspec, aspec, aspec],
-            out_specs=aspec,
+            out_specs=vspec,
             scratch_shapes=[
                 vmem(fw.shape, BF),
                 vmem(rw.shape, BF),
@@ -487,7 +487,7 @@
             in_specs=[vspec],
             out_specs=(vspec, vspec),
             name="place",
-        )(back)
+        )(pltpu.with_memory_space_constraint(back, pltpu.VMEM))
 
     return jax.shard_map(
         body,

time: 30.8 us -> 29.8 us (0.968)
  Pallas kernels: 30 us -> 29 us
    pallas_call x1, Pallas kernels: 1.7 us -> 0.79 us  [body(): pl.pallas_call(place, out_shape=(jax.ShapeDtypeStruct(train.shape, BF), j...]
where the time goes in v4:
time: 29.8 us; the launch traced here: 29.6 us
  Pallas kernels  29 us (97%)
  between operations  0.64 us (2%)
    pallas_call x1, Pallas kernels, body(): pl.pallas_call(functools.partial(kernel, rows_n, feats_n), out_shape=pltp...  28.2 us
    pallas_call x1, Pallas kernels, body(): pl.pallas_call(place, out_shape=(jax.ShapeDtypeStruct(train.shape, BF), j...  0.79 us

profile of v4, /device:TPU:0, one launch (start us, length us, event | category | flops | bytes accessed | tf_op | source)
XLA Modules:
  0.0 29.6 jit_solution(1523394197934754781)
XLA Ops:
  0.6 28.2 %layer.1.back_ref = bf16[4,144,128]{2,1,0:T(8,128)(2,1)S(1)} custom-call(bf16[64,768]{1,0:T(8,128)(2,1)} %train_hbm.1, bf16[32,768]{1,0:T(8,128)(2,1)} %test_hbm.1, bf16[4,192,192]{2,1,0:T(8,128)(2,1)} %fw_hbm.1, bf16[4,192,192]{2,1,0:T(8,128)(2,1)} %rw_hbm.1, bf16[192,768]{1,0:T(8,128)(2,1)} %up_hbm.1, bf16[192,768]{1,0:T(8,128)(2,1)} %bitcast.1), custom_call_target="tpu_custom_call" | custom-call | tf_op jit(solution)/shard_map/layer/pallas_call | solution.py:443
  28.8 0.8 %place.1 = (bf16[64,768]{1,0:T(8,128)(2,1)}, bf16[32,768]{1,0:T(8,128)(2,1)}) custom-call(bf16[4,144,128]{2,1,0:T(8,128)(2,1)S(1)} %layer.1.back_ref), custom_call_target="tpu_custom_call" | custom-call | tf_op jit(solution)/shard_map/place/pallas_call | solution.py:481
